TPU v7x, 256 devices: a whole 4x4x8 slice. The times are simulated.
256 devices in a mesh: mrow: 8 (over y, z_lo), pcol: 32 (over x, z_hi, core).
Axes of the slice: x: 4, y: 4, z: 8 (z_hi: 4, z_lo: 2; z = z_hi * 2 + z_lo), core: 2. Of those that a mesh axis runs over, the one named last changes fastest.
Arguments:
- snapshots: bfloat16 [7424, 8192], P('mrow', 'pcol'), may hold values from -16 to 16
- area_weight: float32 [8192], P('pcol'), may hold values from 0.2 to 1
Outputs:
- gram_tiles: float32 [8, 32, 215296], P('mrow', 'pcol')
All inputs are finite; a program needn't handle non-finite values.
Results may differ from a plain program's by a relative error of at most 0.0003.
Values may be sent and summed in bfloat16 or wider, within the bound.
A program may use at most 64 MiB of HBM per device.

v0:
```python
import jax
import jax.numpy as jnp
from jax import lax
from jax.sharding import Mesh
from jax.sharding import PartitionSpec as P

MEMBERS = 7424
MROW = ("mrow_0", "mrow_1")


def sent_to_all(value, axis):
    copies = jnp.broadcast_to(value, (lax.axis_size(axis), *value.shape))
    return lax.all_to_all(copies, axis, split_axis=0, concat_axis=0, tiled=True)


def of_everyone(value, axis):
    everything = sent_to_all(value, axis)
    return jnp.sum(everything, axis=0)


def gather_axes(value, axes, dim):
    for axis in reversed(axes):
        value = lax.all_gather(value, axis, axis=dim, tiled=True)
    return value


def local(snapshots, area_weight):
    member_rows = snapshots.shape[0]
    ratio = lax.axis_size("pcol") // lax.axis_size(MROW)
    tile = member_rows // ratio
    local_sum = jnp.sum(snapshots.astype(jnp.float32), axis=0)
    ens_mean = of_everyone(local_sum, MROW) / MEMBERS
    anomaly = (
        (snapshots.astype(jnp.float32) - ens_mean[None, :]) * jnp.sqrt(area_weight)[None, :]
    ).astype(jnp.bfloat16)
    contract = (((1,), (1,)), ((), ()))
    every_member = gather_axes(anomaly, MROW, 0)
    col_block = lax.all_to_all(every_member, "pcol", split_axis=0, concat_axis=1, tiled=True)
    gram = lax.dot_general(
        lax.all_gather(anomaly, "pcol", axis=1, tiled=True),
        col_block,
        contract,
        preferred_element_type=jnp.float32,
    )
    gram = gram / (MEMBERS - 1)
    return gram.reshape(1, 1, member_rows * tile)


def solution(mesh):
    torus = Mesh(mesh.devices.reshape(4, 2, mesh.shape["pcol"]), ("mrow_0", "mrow_1", "pcol"))
    return jax.shard_map(
        local,
        mesh=torus,
        in_specs=(P(MROW, "pcol"), P("pcol")),
        out_specs=P(MROW, "pcol", None),
        check_vma=False,
    )
```

profile of v0, /device:TPU:1, one launch (start us, length us, event | category | flops | bytes accessed | tf_op | source)
XLA Modules:
  0.0 288.2 jit_solution(7553588986702876311)
XLA Ops:
  6.5 1.2 convert_reduce_fusion
  7.7 0.6 broadcast_in_dim.2
  8.3 6.4 %all-to-all-start = ((f32[8,1,256]{2,1,0:T(1,128)}), f32[8,1,256]{2,1,0:T(1,128)S(1)}, u32[]{:S(2)}, u32[]{:S(2)}) async-start(f32[8,1,256]{2,1,0:T(1,128)} %broadcast_in_dim.2), calls=%async_computation | async-start | bytes 16384 | tf_op jit(solution)/shard_map/all_to_all | solution.py:13
  14.7 0.0 all-gather.5.cloned.1.call-start
  14.7 0.7 sqrt.3
  15.4 4.3 %all-to-all-done = f32[8,1,256]{2,1,0:T(1,128)S(1)} async-done(((f32[8,1,256]{2,1,0:T(1,128)}), f32[8,1,256]{2,1,0:T(1,128)S(1)}, u32[]{:S(2)}, u32[]{:S(2)}) %all-to-all-start) | async-done | bytes 8224 | tf_op jit(solution)/shard_map/all_to_all | solution.py:13
  19.7 1.1 fusion.1
  20.9 0.0 copy-start
  20.9 11.1 %all_gather.10 = bf16[1856,256]{1,0:T(8,128)(2,1)} all-gather(bf16[928,256]{1,0:T(8,128)(2,1)S(1)} %fusion.1), channel_id=1, replica_groups=mesh['mrow_0'=4,'mrow_1'=2,'pcol'=32] {'mrow_1'}, dimensions={0}, use_global_device_ids=true | all-gather | bytes 1425408 | tf_op jit(solution)/shard_map/all_gather | solution.py:23
  32.0 0.0 all-gather.5.cloned.1.call-update
  32.0 0.0 all-gather.3.cloned.1.call-start
  32.1 0.0 copy-done
  32.1 0.7 all-gather.3.cloned.1.call-update
  32.8 49.1 %all-gather.5.cloned.1.call-done = bf16[7424,256]{1,0:T(8,128)(2,1)} async-done(((bf16[1856,256]{1,0:T(8,128)(2,1)}), bf16[7424,256]{1,0:T(8,128)(2,1)}) %all-gather.5.cloned.1.call-update) | async-done | bytes 3801104 | tf_op jit(solution)/shard_map/all_gather | solution.py:23
  81.9 113.8 %all_to_all.25 = bf16[32,232,256]{2,1,0:T(8,128)(2,1)S(1)} all-to-all(bf16[32,232,256]{2,1,0:T(8,128)(2,1)} %bitcast.7), channel_id=1, replica_groups=mesh['mrow_0'=4,'mrow_1'=2,'pcol'=32] {'pcol'}, dimensions={0} | all-to-all | bytes 7602176 | tf_op jit(solution)/shard_map/all_to_all | solution.py:38
  195.7 2.3 copy.9
  198.0 72.2 %all-gather.3.cloned.1.call-done = bf16[928,8192]{1,0:T(8,128)(2,1)} async-done(((bf16[928,256]{1,0:T(8,128)(2,1)}), bf16[928,8192]{1,0:T(8,128)(2,1)}) %all-gather.3.cloned.1.call-update) | async-done | bytes 15204368 | tf_op jit(solution)/shard_map/all_gather | solution.py:40
  270.3 8.6 %convolution_multiply_fusion = f32[928,232]{1,0:T(8,128)S(1)} fusion(bf16[928,8192]{1,0:T(8,128)(2,1)} %all-gather.3.cloned.1.call-done, bf16[232,8192]{1,0:T(8,128)(2,1)} %bitcast.8), kind=kOutput, calls=%fused_computation | convolution fusion | flops 3527624960 | bytes 19866624 | tf_op jit(solution)/shard_map/dot_general | solution.py:39
  278.8 2.6 reshape.14
  (2 shorter events, 0.0 us)
Async XLA Ops:
  8.3 11.4 %all-to-all-start = ((f32[8,1,256]{2,1,0:T(1,128)}), f32[8,1,256]{2,1,0:T(1,128)S(1)}, u32[]{:S(2)}, u32[]{:S(2)}) async-start(f32[8,1,256]{2,1,0:T(1,128)} %broadcast_in_dim.2), calls=%async_computation | async-start | bytes 16384 | tf_op jit(solution)/shard_map/all_to_all | solution.py:13
  14.7 67.2 %all-gather.5.cloned.1.call-start = ((), (), s32[]{:S(2)}) async-start(), calls=%async_computation.3 | async-start | bytes 4751360 | tf_op jit(solution)/shard_map/all_gather | solution.py:23
  20.9 11.2 %copy-start = (bf16[928,256]{1,0:T(8,128)(2,1)}, bf16[928,256]{1,0:T(8,128)(2,1)S(1)}, u32[]{:S(2)}) copy-start(bf16[928,256]{1,0:T(8,128)(2,1)S(1)} %fusion.1) | copy-start | bytes 1425412
  32.0 238.2 %all-gather.3.cloned.1.call-start = ((), (), s32[]{:S(2)}) async-start(), calls=%async_computation.2 | async-start | bytes 15679488 | tf_op jit(solution)/shard_map/all_gather | solution.py:40
Sparse Core Ops, SparseCore 0:
  32.1 49.6 all-gather.4
  84.3 185.8 all-gather.2
where the time goes:
time: 289 us; the launch traced here: 288 us
  waiting for transfers between devices  126 us (44%)
  blocking collectives  125 us (43%)
  between operations  13.4 us (5%)
  matrix products  8.57 us (3%)
  starting transfers between devices  6.44 us (2%)
  local copies, waits for them, and re-layouts  6.17 us (2%)
    all_to_all x1, blocking collectives, local(): lax.all_to_all(every_member, 'pcol', split_axis=0, concat_axis=1, tiled=T...  114 us
    all_gather x1, waiting for transfers between devices, local(): lax.all_gather(anomaly, 'pcol', axis=1, tiled=True)  72.2 us
    all_gather x1, waiting for transfers between devices, gather_axes(): value = lax.all_gather(value, axis, axis=dim, tiled=True)  49.1 us
    all_gather x1, blocking collectives, gather_axes(): value = lax.all_gather(value, axis, axis=dim, tiled=True)  11.1 us
    dot_general x1, matrix products, local(): lax.dot_general(lax.all_gather(anomaly, 'pcol', axis=1, tiled=True), col_...  8.57 us
    all_to_all x1, starting transfers between devices, sent_to_all(): return lax.all_to_all(copies, axis, split_axis=0, concat_axis=0, tiled=True)  6.36 us
  transfers between devices with their start and end apart: 3, of which 3 were waited for; matrix products, arithmetic and copies ran while one was open for 1% of the time, Pallas kernels for 0%

commit v1 on v0

v1 whole, which is shorter than its diff:
```python
import functools

import jax
import jax.numpy as jnp
from jax import lax
from jax.experimental import pallas as pl
from jax.experimental.pallas import tpu as pltpu
from jax.sharding import PartitionSpec as P

MEMBERS = 7424
MESH = pl.DeviceIdType.MESH


def device(x, y, p, lo, core):
    return (y * 2 + lo, x * 8 + p * 2 + core)


def kernel(
    x_ref, w_ref, out_ref, rows, cols, sums, part, peer,
    row_sem, col_sem, sum_sem, peer_sem, send_sem,
):
    half = x_ref.shape[0] // 2
    tile = half // 2
    me_row, me_col = lax.axis_index("mrow"), lax.axis_index("pcol")
    y, lo = me_row // 2, me_row % 2
    x, p, core = me_col // 8, (me_col // 2) % 4, me_col % 2
    hi, h = p // 2, p % 2

    xp, xm, x2 = (x + 1) % 4, (x + 3) % 4, (x + 2) % 4
    pp, pm, p2 = (p + 1) % 4, (p + 3) % 4, (p + 2) % 4
    yp, ym, y2 = (y + 1) % 4, (y + 3) % 4, (y + 2) % 4
    x_plus, x_minus = device(xp, y, p, lo, core), device(xm, y, p, lo, core)
    z_plus, z_minus = device(x, y, pp, lo, core), device(x, y, pm, lo, core)
    y_plus, y_minus = device(x, yp, p, lo, core), device(x, ym, p, lo, core)
    z_pair = device(x, y, p, 1 - lo, core)
    twin = device(x, y, p, lo, 1 - core)

    turn_lo = ((p + 1) // 2) % 2
    turned = [device(y, x, 2 * lo + s, turn_lo, core) for s in range(2)]
    turn_self = [(x == y) & (2 * lo + s == p) & (turn_lo == lo) for s in range(2)]
    first_p = [lo, 3 - lo]
    turn_from = [device(y, x, q, hi, core) for q in first_p]
    from_self = [(x == y) & (q == p) & (hi == lo) for q in first_p]
    others = [((me_row + d) % 8, me_col) for d in range(1, 8)]

    barrier = pltpu.get_barrier_semaphore()

    def greet(dev):
        pl.semaphore_signal(barrier, inc=1, device_id=dev, device_id_type=MESH)

    for dev in (x_plus, x_minus, z_plus, z_minus, y_plus, y_minus, z_pair, twin, *others):
        greet(dev)
    for s in range(2):
        @pl.when(jnp.logical_not(from_self[s]))
        def _():
            greet(turn_from[s])

    sums[pl.ds(me_row, 1)] = jnp.sum(x_ref[...].astype(jnp.float32), axis=0, keepdims=True)[None]
    stay = jnp.where(turn_self[0], 1, 0) + jnp.where(turn_self[1], 1, 0)
    pl.semaphore_wait(barrier, 17 - stay)

    sends = []

    def send(src, dst, recv_sem, dev):
        n = len(sends)
        copy = pltpu.make_async_remote_copy(
            src_ref=src, dst_ref=dst, send_sem=send_sem.at[n], recv_sem=recv_sem,
            device_id=dev, device_id_type=MESH,
        )
        copy.start()
        sends.append(copy)

    def arrived(ref, recv_sem):
        pltpu.make_async_remote_copy(
            src_ref=ref, dst_ref=ref, send_sem=send_sem.at[0], recv_sem=recv_sem,
            device_id=twin, device_id_type=MESH,
        ).wait_recv()

    for d in range(7):
        slot = sums.at[me_row]
        send(slot, slot, sum_sem.at[me_row], others[d])
    for d in range(1, 8):
        q = (me_row + d) % 8
        arrived(sums.at[q], sum_sem.at[q])
    mean = jnp.sum(sums[...], axis=0) / MEMBERS
    own = x * 4 + p
    rows[pl.ds(own, 1)] = (
        ((x_ref[...].astype(jnp.float32) - mean) * jnp.sqrt(w_ref[...])).astype(jnp.bfloat16)
    )[None]

    def row_half(i, s):
        return rows.at[i, pl.ds(s * half, half)]

    def send_row(i, s, dev):
        send(row_half(i, s), row_half(i, s), row_sem.at[i, s], dev)

    def row_arrived(i, s):
        arrived(row_half(i, s), row_sem.at[i, s])

    def send_col(i, dev):
        send(cols.at[i], cols.at[i], col_sem.at[i], dev)

    def col_arrived(i):
        arrived(cols.at[i], col_sem.at[i])

    turns = []
    for s in range(2):
        n = 64 + s
        copy = pltpu.make_async_remote_copy(
            src_ref=row_half(own, s), dst_ref=cols.at[own], send_sem=send_sem.at[n],
            recv_sem=col_sem.at[own], device_id=turned[s], device_id_type=MESH,
        )
        turns.append(copy)

        @pl.when(jnp.logical_not(turn_self[s]))
        def _():
            copy.start()

        @pl.when(turn_self[s])
        def _():
            cols[pl.ds(own, 1)] = rows[pl.ds(own, 1), s * half:(s + 1) * half]

    def x_sends(i, s):
        send_row(i, s, x_plus)
        send_row(i, s, x_minus)

    def x_forward(q):
        i, j = xm * 4 + q, xp * 4 + q
        row_arrived(i, 0)
        send_row(i, 0, x_plus)
        row_arrived(j, 1)
        send_row(j, 1, x_minus)

    send_row(own, 0, x_plus)
    send_row(own, 1, x_minus)
    send_row(own, 0, z_plus)
    send_row(own, 1, z_minus)
    send_row(own, 1, x_plus)
    send_row(own, 0, x_minus)
    send_row(own, 1, z_plus)
    send_row(own, 0, z_minus)

    x_forward(p)

    firsts = [y * 4 + q for q in first_p]
    for s in range(2):
        @pl.when(jnp.logical_not(from_self[s]))
        def _():
            col_arrived(firsts[s])
    for s in range(2):
        send_col(firsts[s], z_pair)
        send_col(firsts[s], y_plus)
        send_col(firsts[s], y_minus)

    i, j = x * 4 + pm, x * 4 + pp
    row_arrived(i, 0)
    send_row(i, 0, z_plus)
    x_sends(i, 0)
    row_arrived(j, 1)
    send_row(j, 1, z_minus)
    x_sends(j, 1)
    row_arrived(i, 1)
    x_sends(i, 1)
    row_arrived(j, 0)
    x_sends(j, 0)

    seconds = [y * 4 + q for q in (1 - lo, 2 + lo)]
    for s in range(2):
        col_arrived(seconds[s])
        send_col(seconds[s], y_plus)
        send_col(seconds[s], y_minus)

    col_arrived(ym * 4 + first_p[0])
    send_col(ym * 4 + first_p[0], y_plus)
    col_arrived(yp * 4 + first_p[1])
    send_col(yp * 4 + first_p[1], y_minus)

    x_forward(pm)
    x_forward(pp)

    k = x * 4 + p2
    row_arrived(k, 0)
    x_sends(k, 0)
    row_arrived(k, 1)
    x_sends(k, 1)

    col_arrived(ym * 4 + 1 - lo)
    send_col(ym * 4 + 1 - lo, y_plus)
    col_arrived(yp * 4 + 2 + lo)
    send_col(yp * 4 + 2 + lo, y_minus)

    x_forward(p2)

    for i in (ym * 4 + first_p[1], yp * 4 + first_p[0], ym * 4 + 2 + lo, yp * 4 + 1 - lo):
        col_arrived(i)
    for q in range(4):
        col_arrived(y2 * 4 + q)

    contract = (((1,), (1,)), ((), ()))

    def add(i, first):
        block = rows[i]
        column = cols[i]
        for c in range(2):
            term = lax.dot_general(
                block, column[c * tile:(c + 1) * tile], contract, preferred_element_type=jnp.float32
            )
            if first:
                part[c] = term
            else:
                part[c] += term

    add(own, True)
    for q in (pm, pp, p2):
        add(x * 4 + q, False)

    def per_p(step, _):
        q = (p + jnp.where(step == 0, 0, jnp.where(step == 1, 3, jnp.where(step == 2, 1, 2)))) % 4
        row_arrived(xm * 4 + q, 1)
        add(xm * 4 + q, False)
        row_arrived(xp * 4 + q, 0)
        add(xp * 4 + q, False)
        row_arrived(x2 * 4 + q, 0)
        row_arrived(x2 * 4 + q, 1)
        add(x2 * 4 + q, False)
        return 0

    lax.fori_loop(0, 4, per_p, 0)

    send(part.at[1 - core], peer, peer_sem, twin)
    arrived(peer, peer_sem)
    out_ref[...] = (part[core] + peer[...]) / (MEMBERS - 1)

    for copy in sends:
        copy.wait_send()
    for s in range(2):
        @pl.when(jnp.logical_not(turn_self[s]))
        def _():
            turns[s].wait_send()


def local(snapshots, area_weight):
    members, points = snapshots.shape
    tile = members // 4
    vmem = pl.BlockSpec(memory_space=pltpu.VMEM)
    gram = pl.pallas_call(
        kernel,
        out_shape=jax.ShapeDtypeStruct((members, tile), jnp.float32),
        in_specs=[vmem, vmem],
        out_specs=vmem,
        scratch_shapes=[
            pltpu.VMEM((16, members, points), jnp.bfloat16),
            pltpu.VMEM((16, members // 2, points), jnp.bfloat16),
            pltpu.VMEM((8, 1, points), jnp.float32),
            pltpu.VMEM((2, members, tile), jnp.float32),
            pltpu.VMEM((members, tile), jnp.float32),
            pltpu.SemaphoreType.DMA((16, 2)),
            pltpu.SemaphoreType.DMA((16,)),
            pltpu.SemaphoreType.DMA((8,)),
            pltpu.SemaphoreType.DMA,
            pltpu.SemaphoreType.DMA((66,)),
        ],
        compiler_params=pltpu.CompilerParams(collective_id=0, has_side_effects=True),
    )(snapshots, area_weight.reshape(1, points))
    return gram.reshape(1, 1, members * tile)


def solution(mesh):
    return jax.shard_map(
        local,
        mesh=mesh,
        in_specs=(P("mrow", "pcol"), P("pcol")),
        out_specs=P("mrow", "pcol", None),
        check_vma=False,
    )
```

time: 289 us -> 111 us (0.38)
  waiting for transfers between devices: 126 us -> 0 us
  blocking collectives: 125 us -> 0 us
  Pallas kernels: 0 us -> 107 us
  between operations: 13.4 us -> 0.01 us
  matrix products: 8.57 us -> 0 us
  starting transfers between devices: 6.44 us -> 0 us
    all_gather x2 -> x0, waiting for transfers between devices: 121 us -> none  [the longest x1 72.2 us: local(): lax.all_gather(anomaly, 'pcol', axis=1, tiled=True)]
    all_to_all x1 -> x0, blocking collectives: 114 us -> none  [local(): lax.all_to_all(every_member, 'pcol', split_axis=0, concat_axis=1, tiled=T...]
    pallas_call x0 -> x1, Pallas kernels: none -> 107 us  [local(): pl.pallas_call(kernel, out_shape=jax.ShapeDtypeStruct((members, tile), jn...]
    all_gather x1 -> x0, blocking collectives: 11.1 us -> none  [gather_axes(): value = lax.all_gather(value, axis, axis=dim, tiled=True)]
    dot_general x1 -> x0, matrix products: 8.57 us -> none  [local(): lax.dot_general(lax.all_gather(anomaly, 'pcol', axis=1, tiled=True), col_...]
    all_to_all x1 -> x0, starting transfers between devices: 6.36 us -> none  [sent_to_all(): return lax.all_to_all(copies, axis, split_axis=0, concat_axis=0, tiled=True)]
    all_to_all x1 -> x0, waiting for transfers between devices: 4.31 us -> none  [sent_to_all(): return lax.all_to_all(copies, axis, split_axis=0, concat_axis=0, tiled=True)]
  transfers between devices with their start and end apart: 3 -> 0, of which waited for: 3 -> 0; matrix products, arithmetic and copies ran while one was open for 1% -> 0% of each run, Pallas kernels for 0% -> 0%
where the time goes in v1:
time: 111 us
  Pallas kernels  107 us (96%)
  local copies, waits for them, and re-layouts  3.77 us (3%)
    pallas_call x1, Pallas kernels, local(): pl.pallas_call(kernel, out_shape=jax.ShapeDtypeStruct((members, tile), jn...  107 us
    reshape x1, local copies, waits for them, and re-layouts, local(): return gram.reshape(1, 1, members * tile)  3.77 us

profile of v1, /device:TPU:1, one launch (start us, length us, event | category | flops | bytes accessed | tf_op | source)
XLA Modules:
  0.0 111.2 jit_solution(11153997813411344242)
XLA Ops:
  0.0 107.4 %shard_map.28 = f32[928,232]{1,0:T(8,128)} custom-call(bf16[928,256]{1,0:T(8,128)(2,1)} %x_ref.1, f32[1,256]{1,0:T(1,128)} %bitcast.1), custom_call_target="tpu_custom_call" | custom-call | tf_op jit(solution)/shard_map/pallas_call | solution.py:246
  107.4 3.8 %reshape.7 = f32[1,1,215296]{2,1,0:T(1,128)} reshape(f32[928,232]{1,0:T(8,128)} %shard_map.28) | data formatting | bytes 1722368 | tf_op jit(solution)/shard_map/reshape | solution.py:265

commit v2 on v0

v2 whole, which is shorter than its diff:
```python
import jax
import jax.numpy as jnp
from jax import lax
from jax.experimental import pallas as pl
from jax.experimental.pallas import tpu as pltpu
from jax.sharding import PartitionSpec as P

MEMBERS = 7424
MESH = pl.DeviceIdType.MESH
SENDS = 80


def device(x, y, p, lo, core):
    return (y * 2 + lo, x * 8 + p * 2 + core)


def kernel(
    x_ref, w_ref, out_ref, rows, cols, anom, canom, passing, sums, ysums, table, part, peer,
    row_sem, col_sem, pass_sem, sum_sem, ysum_sem, ztab_sem, xtab_sem, peer_sem, send_sem,
):
    half = x_ref.shape[0] // 2
    tile = half // 2
    me_row, me_col = lax.axis_index("mrow"), lax.axis_index("pcol")
    y, lo = me_row // 2, me_row % 2
    x, p, core = me_col // 8, (me_col // 2) % 4, me_col % 2
    hi = p // 2

    xp, xm, x2 = (x + 1) % 4, (x + 3) % 4, (x + 2) % 4
    pp, pm, p2 = (p + 1) % 4, (p + 3) % 4, (p + 2) % 4
    yp, ym, y2 = (y + 1) % 4, (y + 3) % 4, (y + 2) % 4
    x_plus, x_minus, x_far = (device(v, y, p, lo, core) for v in (xp, xm, x2))
    z_plus, z_minus, z_far = (device(x, y, v, lo, core) for v in (pp, pm, p2))
    y_plus, y_minus, y_far = (device(x, v, p, lo, core) for v in (yp, ym, y2))
    z_pair = device(x, y, p, 1 - lo, core)
    twin = device(x, y, p, lo, 1 - core)
    own = x * 4 + p
    diagonal = x == y

    def origin(v):
        return (v + 2 * ((x + v + 1) % 2)) % 4


    turn_lo = ((p + 1) // 2) % 2
    turned = [device(x, y, 2 * lo + s, turn_lo, core) for s in range(2)]
    stays = [(2 * lo + s == p) & (turn_lo == lo) for s in range(2)]
    moves = [jnp.logical_not(v) for v in stays]
    first_p = [lo, 3 - lo]
    second_p = [1 - lo, 2 + lo]
    turn_from = [device(x, y, q, hi, core) for q in first_p]
    from_here = [(q == p) & (hi == lo) for q in first_p]

    barrier = pltpu.get_barrier_semaphore()

    def greet(dev):
        pl.semaphore_signal(barrier, inc=1, device_id=dev, device_id_type=MESH)

    for dev in (x_plus, x_minus, x_far, z_plus, z_minus, z_far, y_plus, y_minus, y_far, z_pair, twin):
        greet(dev)
    for s in range(2):
        @pl.when(jnp.logical_not(from_here[s]))
        def _():
            greet(turn_from[s])

    sums[pl.ds(0, 1)] = jnp.sum(x_ref[...].astype(jnp.float32), axis=0, keepdims=True)[None]
    pl.semaphore_wait(barrier, 13 - jnp.where(stays[0], 1, 0) - jnp.where(stays[1], 1, 0))

    sends = []
    count = [0]

    def copy_to(src, dst, recv_sem, dev, n):
        return pltpu.make_async_remote_copy(
            src_ref=src, dst_ref=dst, send_sem=send_sem.at[n], recv_sem=recv_sem,
            device_id=dev, device_id_type=MESH,
        )

    def new_sem():
        count[0] += 1
        return count[0] - 1

    def send(src, dst, recv_sem, dev):
        copy = copy_to(src, dst, recv_sem, dev, new_sem())
        copy.start()
        sends.append(copy)

    def arrived(ref, recv_sem):
        copy_to(ref, ref, recv_sem, twin, 0).wait_recv()

    def row_half(i, s):
        return rows.at[i, pl.ds(s * half, half)]

    def own_half(s):
        return x_ref.at[pl.ds(s * half, half)]

    def send_own(s, dev):
        send(own_half(s), row_half(own, s), row_sem.at[own, s], dev)

    def send_row(i, s, dev):
        send(row_half(i, s), row_half(i, s), row_sem.at[i, s], dev)

    def row_arrived(i, s):
        arrived(row_half(i, s), row_sem.at[i, s])

    def send_col(i, dev):
        send(cols.at[i], cols.at[i], col_sem.at[i], dev)

    def col_arrived(i):
        arrived(cols.at[i], col_sem.at[i])

    def x_sends(i, s):
        send_row(i, s, x_plus)
        send_row(i, s, x_minus)

    def x_forward(q):
        i, j = xm * 4 + q, xp * 4 + q
        row_arrived(i, 0)
        send_row(i, 0, x_plus)
        row_arrived(j, 1)
        send_row(j, 1, x_minus)

    pushes = []

    def push(src, i, s, dev):
        n = new_sem()

        @pl.when(diagonal & stays[s])
        def _():
            copy_to(src, cols.at[i], col_sem.at[i], dev, n).start()

        @pl.when(diagonal & moves[s])
        def _():
            copy_to(src, passing.at[s], pass_sem.at[s], dev, n).start()

        pushes.append((src, n))

    def push_row(v, s, dev):
        push(row_half(v * 4 + p, s), v * 4 + p, s, dev)

    turns = []

    def turn_on(s):
        n = new_sem()
        i = origin(y) * 4 + p

        @pl.when(diagonal & moves[s])
        def _():
            copy_to(row_half(x2 * 4 + p, s), cols.at[i], col_sem.at[i], turned[s], n).start()

        @pl.when(diagonal & stays[s])
        def _():
            cols[pl.ds(i, 1)] = rows[pl.ds(x2 * 4 + p, 1), s * half:(s + 1) * half]

        @pl.when(jnp.logical_not(diagonal) & moves[s])
        def _():
            arrived(passing.at[s], pass_sem.at[s])
            copy_to(passing.at[s], cols.at[i], col_sem.at[i], turned[s], n).start()

        turns.append((s, n))

    def to_anomaly(block, i):
        entry = table[i]
        return ((block.astype(jnp.float32) - entry[0:1]) * entry[1:2]).astype(jnp.bfloat16)

    def row_anomaly(i):
        anom[pl.ds(i, 1)] = to_anomaly(rows[i], i)[None]

    def col_anomaly(i):
        canom[pl.ds(i, 1)] = to_anomaly(cols[i], i)[None]

    contract = (((1,), (1,)), ((), ()))

    def add(i):
        block = anom[i]
        column = canom[i]
        for c in range(2):
            part[c] += lax.dot_general(
                block, column[c * tile:(c + 1) * tile], contract, preferred_element_type=jnp.float32
            )

    def nth(step):
        return (p + jnp.where(step == 0, 3, jnp.where(step == 1, 1, 2))) % 4

    def start():
        send(sums.at[0], sums.at[1], sum_sem, z_pair)
        send_own(0, x_plus)
        send_own(1, x_minus)
        send_own(0, z_plus)
        send_own(1, z_minus)
        push(own_half(0), own, 0, y_far)
        push(own_half(1), own, 1, y_far)

    def means():
        arrived(sums.at[1], sum_sem)
        ysums[pl.ds(y, 1)] = (sums[0] + sums[1])[None]
        for dev in (y_plus, y_minus, y_far):
            send(ysums.at[y], ysums.at[y], ysum_sem.at[y], dev)
        send_own(1, x_plus)
        send_own(0, x_minus)
        for v in (yp, ym, y2):
            arrived(ysums.at[v], ysum_sem.at[v])
        mean = jnp.sum(ysums[...], axis=0) / MEMBERS
        table[pl.ds(own, 1)] = jnp.concatenate([mean, jnp.sqrt(w_ref[...])], axis=0)[None]
        for dev in (z_plus, z_minus, z_far):
            send(table.at[own], table.at[own], ztab_sem.at[p], dev)
        send_own(1, z_plus)
        send_own(0, z_minus)

    def near_push():
        push_row(xm, 0, y_minus)
        push_row(xp, 1, y_plus)

    def z_first():
        i, j = x * 4 + pm, x * 4 + pp
        row_arrived(i, 0)
        x_sends(i, 0)
        row_arrived(j, 1)
        x_sends(j, 1)

    def z_fwd():
        send_row(x * 4 + pm, 0, z_plus)
        send_row(x * 4 + pp, 1, z_minus)

    def near_push2():
        row_arrived(xm * 4 + p, 1)
        push_row(xm, 1, y_minus)
        row_arrived(xp * 4 + p, 0)
        push_row(xp, 0, y_plus)

    def tables():
        for q in (pp, pm, p2):
            arrived(table.at[x * 4 + q], ztab_sem.at[q])
        group = table.at[pl.ds(x * 4, 4)]
        for dev in (x_plus, x_minus, x_far):
            send(group, group, xtab_sem.at[x], dev)

    def far_rows():
        row_arrived(x2 * 4 + p, 0)
        row_arrived(x2 * 4 + p, 1)

    def z_second():
        i, j = x * 4 + pm, x * 4 + pp
        row_arrived(i, 1)
        x_sends(i, 1)
        row_arrived(j, 0)
        x_sends(j, 0)

    def turn_all():
        turn_on(0)
        turn_on(1)

    def x_fwd0():
        x_forward(p)

    def x_fwd1():
        x_forward(pm)
        x_forward(pp)

    def x_fwd2():
        x_forward(p2)

    def firsts():
        for s in range(2):
            i = origin(y) * 4 + first_p[s]

            @pl.when(jnp.logical_not(from_here[s] & diagonal))
            def _():
                col_arrived(i)

            send_col(i, z_pair)
            send_col(i, y_plus)
            send_col(i, y_minus)

    def z_far_rows():
        k = x * 4 + p2
        for s in range(2):
            row_arrived(k, s)
            x_sends(k, s)

    def seconds():
        for q in second_p:
            col_arrived(origin(y) * 4 + q)
            send_col(origin(y) * 4 + q, y_plus)
            send_col(origin(y) * 4 + q, y_minus)

    def tables2():
        for v in (xp, xm, x2):
            arrived(table.at[pl.ds(v * 4, 4)], xtab_sem.at[v])

    def y_fwd(pair):
        a, b = pair
        col_arrived(origin(ym) * 4 + a)
        send_col(origin(ym) * 4 + a, y_plus)
        col_arrived(origin(yp) * 4 + b)
        send_col(origin(yp) * 4 + b, y_minus)

    def y_fwd1():
        y_fwd(first_p)

    def y_fwd2():
        y_fwd(second_p)

    def near_anomalies():
        anom[pl.ds(own, 1)] = to_anomaly(x_ref[...], own)[None]
        part[...] = jnp.zeros_like(part)
        for v in (xm, xp, x2):
            row_anomaly(v * 4 + p)

    def rest(step, _):
        q = nth(step)
        row_arrived(xm * 4 + q, 1)
        row_arrived(xp * 4 + q, 0)
        row_arrived(x2 * 4 + q, 0)
        row_arrived(x2 * 4 + q, 1)
        for v in (x, xm, xp, x2):
            row_anomaly(v * 4 + q)
        return 0

    def rest2():
        lax.fori_loop(0, 2, rest, 0)

    def rest_cols():
        for a, b in (first_p, second_p):
            col_arrived(origin(ym) * 4 + b)
            col_arrived(origin(yp) * 4 + a)
        for q in range(4):
            col_arrived(origin(y2) * 4 + q)

    def compute():
        def col_all(i, _):
            col_anomaly(i)
            return 0

        lax.fori_loop(0, 16, col_all, 0)

        def products(n, _):
            q = (p + 3 + n // 4) % 4
            add((n % 4) * 4 + q)
            return 0

        lax.fori_loop(0, 12, products, 0)
        lax.fori_loop(2, 3, rest, 0)
        lax.fori_loop(12, 16, products, 0)

    for step in (
        start, means, x_fwd0, near_push, z_first, near_push2, tables, far_rows, turn_all, z_second, z_fwd,
        firsts, x_fwd1, z_far_rows, seconds, tables2, near_anomalies, y_fwd1, y_fwd2, x_fwd2, rest2,
        rest_cols, compute,
    ):
        step()

    send(part.at[1 - core], peer, peer_sem, twin)
    arrived(peer, peer_sem)
    out_ref[...] = (part[core] + peer[...]) / (MEMBERS - 1)

    for copy in sends:
        copy.wait_send()
    for src, n in pushes:
        @pl.when(diagonal)
        def _():
            copy_to(src, src, pass_sem.at[0], twin, n).wait_send()
    for s, n in turns:
        @pl.when(moves[s])
        def _():
            copy_to(passing.at[s], passing.at[s], pass_sem.at[0], twin, n).wait_send()


def local(snapshots, area_weight):
    members, points = snapshots.shape
    tile = members // 4
    vmem = pl.BlockSpec(memory_space=pltpu.VMEM)
    dma = pltpu.SemaphoreType.DMA
    gram = pl.pallas_call(
        kernel,
        out_shape=jax.ShapeDtypeStruct((members, tile), jnp.float32),
        in_specs=[vmem, vmem],
        out_specs=vmem,
        scratch_shapes=[
            pltpu.VMEM((16, members, points), jnp.bfloat16),
            pltpu.VMEM((16, members // 2, points), jnp.bfloat16),
            pltpu.VMEM((16, members, points), jnp.bfloat16),
            pltpu.VMEM((16, members // 2, points), jnp.bfloat16),
            pltpu.VMEM((2, members // 2, points), jnp.bfloat16),
            pltpu.VMEM((2, 1, points), jnp.float32),
            pltpu.VMEM((4, 1, points), jnp.float32),
            pltpu.VMEM((16, 2, points), jnp.float32),
            pltpu.VMEM((2, members, tile), jnp.float32),
            pltpu.VMEM((members, tile), jnp.float32),
            dma((16, 2)),
            dma((16,)),
            dma((2,)),
            dma,
            dma((4,)),
            dma((4,)),
            dma((4,)),
            dma,
            dma((SENDS,)),
        ],
        compiler_params=pltpu.CompilerParams(collective_id=0, has_side_effects=True),
    )(snapshots, area_weight.reshape(1, points))
    return gram.reshape(1, 1, members * tile)


def solution(mesh):
    return jax.shard_map(
        local,
        mesh=mesh,
        in_specs=(P("mrow", "pcol"), P("pcol")),
        out_specs=P("mrow", "pcol", None),
        check_vma=False,
    )
```

time: 289 us -> 104 us (0.36)
  waiting for transfers between devices: 126 us -> 0 us
  blocking collectives: 125 us -> 0 us
  Pallas kernels: 0 us -> 100 us
  between operations: 13.4 us -> 0.01 us
  matrix products: 8.57 us -> 0 us
  starting transfers between devices: 6.44 us -> 0 us
    all_gather x2 -> x0, waiting for transfers between devices: 121 us -> none  [the longest x1 72.2 us: local(): lax.all_gather(anomaly, 'pcol', axis=1, tiled=True)]
    all_to_all x1 -> x0, blocking collectives: 114 us -> none  [local(): lax.all_to_all(every_member, 'pcol', split_axis=0, concat_axis=1, tiled=T...]
    pallas_call x0 -> x1, Pallas kernels: none -> 100 us  [local(): pl.pallas_call(kernel, out_shape=jax.ShapeDtypeStruct((members, tile), jn...]
    all_gather x1 -> x0, blocking collectives: 11.1 us -> none  [gather_axes(): value = lax.all_gather(value, axis, axis=dim, tiled=True)]
    dot_general x1 -> x0, matrix products: 8.57 us -> none  [local(): lax.dot_general(lax.all_gather(anomaly, 'pcol', axis=1, tiled=True), col_...]
    all_to_all x1 -> x0, starting transfers between devices: 6.36 us -> none  [sent_to_all(): return lax.all_to_all(copies, axis, split_axis=0, concat_axis=0, tiled=True)]
    all_to_all x1 -> x0, waiting for transfers between devices: 4.31 us -> none  [sent_to_all(): return lax.all_to_all(copies, axis, split_axis=0, concat_axis=0, tiled=True)]
  transfers between devices with their start and end apart: 3 -> 0, of which waited for: 3 -> 0; matrix products, arithmetic and copies ran while one was open for 1% -> 0% of each run, Pallas kernels for 0% -> 0%
where the time goes in v2:
time: 104 us
  Pallas kernels  100 us (96%)
  local copies, waits for them, and re-layouts  3.77 us (4%)
    pallas_call x1, Pallas kernels, local(): pl.pallas_call(kernel, out_shape=jax.ShapeDtypeStruct((members, tile), jn...  100 us
    reshape x1, local copies, waits for them, and re-layouts, local(): return gram.reshape(1, 1, members * tile)  3.77 us

profile of v2, /device:TPU:1, one launch (start us, length us, event | category | flops | bytes accessed | tf_op | source)
XLA Modules:
  0.0 103.8 jit_solution(13105803458992881396)
XLA Ops:
  0.0 100.0 %shard_map.28 = f32[928,232]{1,0:T(8,128)} custom-call(bf16[928,256]{1,0:T(8,128)(2,1)} %x_ref.1, f32[1,256]{1,0:T(1,128)} %bitcast.1), custom_call_target="tpu_custom_call" | custom-call | tf_op jit(solution)/shard_map/pallas_call | solution.py:371
  100.0 3.8 %reshape.7 = f32[1,1,215296]{2,1,0:T(1,128)} reshape(f32[928,232]{1,0:T(8,128)} %shard_map.28) | data formatting | bytes 1722368 | tf_op jit(solution)/shard_map/reshape | solution.py:399

commit v3 on v2

--- a/solution.py
+++ b/solution.py
@@ -15,7 +15,7 @@
 
 
 def kernel(
-    x_ref, w_ref, out_ref, rows, cols, anom, canom, passing, sums, ysums, table, part, peer,
+    x_ref, w_ref, out_ref, rows, cols, passing, sums, ysums, table, part, peer,
     row_sem, col_sem, pass_sem, sum_sem, ysum_sem, ztab_sem, xtab_sem, peer_sem, send_sem,
 ):
     half = x_ref.shape[0] // 2
@@ -40,12 +40,12 @@
         return (v + 2 * ((x + v + 1) % 2)) % 4
 
 
-    turn_lo = ((p + 1) // 2) % 2
-    turned = [device(x, y, 2 * lo + s, turn_lo, core) for s in range(2)]
-    stays = [(2 * lo + s == p) & (turn_lo == lo) for s in range(2)]
+    turn_lo = [((lo + s - p) % 4) // 2 for s in range(2)]
+    turned = [device(x, y, 2 * lo + s, turn_lo[s], core) for s in range(2)]
+    stays = [2 * lo + s == p for s in range(2)]
     moves = [jnp.logical_not(v) for v in stays]
-    first_p = [lo, 3 - lo]
-    second_p = [1 - lo, 2 + lo]
+    first_p = [(p - hi - 3 * lo) % 4, (p - hi - 1 - lo) % 4]
+    second_p = [(p - hi - 3 * (1 - lo)) % 4, (p - hi - 2 + lo) % 4]
     turn_from = [device(x, y, q, hi, core) for q in first_p]
     from_here = [(q == p) & (hi == lo) for q in first_p]
 
@@ -62,7 +62,7 @@
             greet(turn_from[s])
 
     sums[pl.ds(0, 1)] = jnp.sum(x_ref[...].astype(jnp.float32), axis=0, keepdims=True)[None]
-    pl.semaphore_wait(barrier, 13 - jnp.where(stays[0], 1, 0) - jnp.where(stays[1], 1, 0))
+    pl.semaphore_wait(barrier, 13 - jnp.where(hi == lo, 1, 0))
 
     sends = []
     count = [0]
@@ -160,24 +160,13 @@
         entry = table[i]
         return ((block.astype(jnp.float32) - entry[0:1]) * entry[1:2]).astype(jnp.bfloat16)
 
-    def row_anomaly(i):
-        anom[pl.ds(i, 1)] = to_anomaly(rows[i], i)[None]
-
-    def col_anomaly(i):
-        canom[pl.ds(i, 1)] = to_anomaly(cols[i], i)[None]
-
     contract = (((1,), (1,)), ((), ()))
 
-    def add(i):
-        block = anom[i]
-        column = canom[i]
-        for c in range(2):
-            part[c] += lax.dot_general(
-                block, column[c * tile:(c + 1) * tile], contract, preferred_element_type=jnp.float32
-            )
-
-    def nth(step):
-        return (p + jnp.where(step == 0, 3, jnp.where(step == 1, 1, 2))) % 4
+    def nth(n, values):
+        value = values[0]
+        for k in range(1, len(values)):
+            value = jnp.where(n == k, values[k], value)
+        return value
 
     def start():
         send(sums.at[0], sums.at[1], sum_sem, z_pair)
@@ -185,16 +174,18 @@
         send_own(1, x_minus)
         send_own(0, z_plus)
         send_own(1, z_minus)
-        push(own_half(0), own, 0, y_far)
-        push(own_half(1), own, 1, y_far)
-
-    def means():
+        send_own(1, x_plus)
+        send_own(0, x_minus)
+
+    def pair_sums():
         arrived(sums.at[1], sum_sem)
         ysums[pl.ds(y, 1)] = (sums[0] + sums[1])[None]
         for dev in (y_plus, y_minus, y_far):
             send(ysums.at[y], ysums.at[y], ysum_sem.at[y], dev)
-        send_own(1, x_plus)
-        send_own(0, x_minus)
+        push(own_half(0), own, 0, y_far)
+        push(own_half(1), own, 1, y_far)
+
+    def means():
         for v in (yp, ym, y2):
             arrived(ysums.at[v], ysum_sem.at[v])
         mean = jnp.sum(ysums[...], axis=0) / MEMBERS
@@ -243,8 +234,10 @@
         row_arrived(j, 0)
         x_sends(j, 0)
 
-    def turn_all():
+    def turn0():
         turn_on(0)
+
+    def turn1():
         turn_on(1)
 
     def x_fwd0():
@@ -257,17 +250,22 @@
     def x_fwd2():
         x_forward(p2)
 
-    def firsts():
-        for s in range(2):
-            i = origin(y) * 4 + first_p[s]
-
-            @pl.when(jnp.logical_not(from_here[s] & diagonal))
-            def _():
-                col_arrived(i)
-
-            send_col(i, z_pair)
-            send_col(i, y_plus)
-            send_col(i, y_minus)
+    def first(s):
+        i = origin(y) * 4 + first_p[s]
+
+        @pl.when(jnp.logical_not(from_here[s] & diagonal))
+        def _():
+            col_arrived(i)
+
+        send_col(i, z_pair)
+        send_col(i, y_plus)
+        send_col(i, y_minus)
+
+    def first0():
+        first(0)
+
+    def first1():
+        first(1)
 
     def z_far_rows():
         k = x * 4 + p2
@@ -275,75 +273,94 @@
             row_arrived(k, s)
             x_sends(k, s)
 
-    def seconds():
-        for q in second_p:
-            col_arrived(origin(y) * 4 + q)
-            send_col(origin(y) * 4 + q, y_plus)
-            send_col(origin(y) * 4 + q, y_minus)
+    def second(s):
+        i = origin(y) * 4 + second_p[s]
+        col_arrived(i)
+        send_col(i, y_plus)
+        send_col(i, y_minus)
+
+    def second0():
+        second(0)
+
+    def second1():
+        second(1)
 
     def tables2():
         for v in (xp, xm, x2):
             arrived(table.at[pl.ds(v * 4, 4)], xtab_sem.at[v])
 
-    def y_fwd(pair):
-        a, b = pair
-        col_arrived(origin(ym) * 4 + a)
-        send_col(origin(ym) * 4 + a, y_plus)
-        col_arrived(origin(yp) * 4 + b)
-        send_col(origin(yp) * 4 + b, y_minus)
-
-    def y_fwd1():
-        y_fwd(first_p)
-
-    def y_fwd2():
-        y_fwd(second_p)
-
-    def near_anomalies():
-        anom[pl.ds(own, 1)] = to_anomaly(x_ref[...], own)[None]
-        part[...] = jnp.zeros_like(part)
-        for v in (xm, xp, x2):
-            row_anomaly(v * 4 + p)
-
-    def rest(step, _):
-        q = nth(step)
+    def y_fwd():
+        i, j = origin(ym) * 4 + first_p[0], origin(yp) * 4 + first_p[1]
+        col_arrived(i)
+        send_col(i, y_plus)
+        col_arrived(j)
+        send_col(j, y_minus)
+
+    def far_pass():
+        for q in first_p:
+            col_arrived(origin(y2) * 4 + q)
+            send_col(origin(y2) * 4 + q, z_pair)
+
+    def rows_rest(q):
         row_arrived(xm * 4 + q, 1)
         row_arrived(xp * 4 + q, 0)
         row_arrived(x2 * 4 + q, 0)
         row_arrived(x2 * 4 + q, 1)
-        for v in (x, xm, xp, x2):
-            row_anomaly(v * 4 + q)
-        return 0
-
-    def rest2():
-        lax.fori_loop(0, 2, rest, 0)
-
-    def rest_cols():
-        for a, b in (first_p, second_p):
-            col_arrived(origin(ym) * 4 + b)
-            col_arrived(origin(yp) * 4 + a)
-        for q in range(4):
-            col_arrived(origin(y2) * 4 + q)
-
-    def compute():
-        def col_all(i, _):
-            col_anomaly(i)
+
+    f0, f1 = first_p
+    s0, s1 = second_p
+    order = (
+        (y, f0), (y, f1), (y, s0), (y, s1),
+        (ym, f0), (yp, f1), (ym, f1), (yp, f0), (y2, f0), (y2, f1),
+        (ym, s0), (yp, s0), (ym, s1), (yp, s1), (y2, s0), (y2, s1),
+    )
+
+    def products(first, last, wanted, wait):
+        def product(n, _):
+            i = nth(n, [origin(v) * 4 + q for v, q in order[first:last]])
+            if wait:
+                @pl.when((n == 2) | (n == 3) if first == 4 else n >= 0)
+                def _():
+                    col_arrived(i)
+
+            @pl.when(wanted(i % 4))
+            def _():
+                block = to_anomaly(rows[i], i)
+                column = to_anomaly(cols[i], i)
+                for c in range(2):
+                    part[c] += lax.dot_general(
+                        block, column[c * tile:(c + 1) * tile], contract,
+                        preferred_element_type=jnp.float32,
+                    )
             return 0
 
-        lax.fori_loop(0, 16, col_all, 0)
-
-        def products(n, _):
-            q = (p + 3 + n // 4) % 4
-            add((n % 4) * 4 + q)
-            return 0
-
-        lax.fori_loop(0, 12, products, 0)
-        lax.fori_loop(2, 3, rest, 0)
-        lax.fori_loop(12, 16, products, 0)
+        lax.fori_loop(0, last - first, product, 0)
+
+    def near(q):
+        return q != p2
+
+    def far(q):
+        return q == p2
+
+    def prod_a():
+        rows_rest(pm)
+        rows_rest(pp)
+        rows[pl.ds(own, 1)] = x_ref[...][None]
+        part[...] = jnp.zeros_like(part)
+        products(0, 4, near, False)
+
+    def prod_b():
+        products(4, 10, near, True)
+
+    def prod_c():
+        products(10, 16, near, True)
+
+    def prod_d():
+        rows_rest(p2)
+        products(0, 16, far, False)
 
     for step in (
-        start, means, x_fwd0, near_push, z_first, near_push2, tables, far_rows, turn_all, z_second, z_fwd,
-        firsts, x_fwd1, z_far_rows, seconds, tables2, near_anomalies, y_fwd1, y_fwd2, x_fwd2, rest2,
-        rest_cols, compute,
+        start, pair_sums, means, x_fwd0, near_push, near_push2, z_first, far_rows, turn0, turn1, tables, z_second, z_fwd, first0, first1, x_fwd1, y_fwd, z_far_rows, second0, second1, tables2, far_pass, prod_a, x_fwd2, prod_b, prod_c, prod_d,
     ):
         step()
 
@@ -374,8 +391,6 @@
         in_specs=[vmem, vmem],
         out_specs=vmem,
         scratch_shapes=[
-            pltpu.VMEM((16, members, points), jnp.bfloat16),
-            pltpu.VMEM((16, members // 2, points), jnp.bfloat16),
             pltpu.VMEM((16, members, points), jnp.bfloat16),
             pltpu.VMEM((16, members // 2, points), jnp.bfloat16),
             pltpu.VMEM((2, members // 2, points), jnp.bfloat16),

time: 104 us -> 90.5 us (0.87)
  the two profiles are of different devices: /device:TPU:1 before, /device:TPU:97 now
where the time goes in v3:
time: 90.5 us; the launch traced here: 90.4 us
  Pallas kernels  86.6 us (96%)
  local copies, waits for them, and re-layouts  3.77 us (4%)
    pallas_call x1, Pallas kernels, local(): pl.pallas_call(kernel, out_shape=jax.ShapeDtypeStruct((members, tile), jn...  86.6 us
    reshape x1, local copies, waits for them, and re-layouts, local(): return gram.reshape(1, 1, members * tile)  3.77 us

profile of v3, /device:TPU:97, one launch (start us, length us, event | category | flops | bytes accessed | tf_op | source)
XLA Modules:
  0.0 90.4 jit_solution(15089968223571888723)
XLA Ops:
  0.0 86.6 %shard_map.28 = f32[928,232]{1,0:T(8,128)} custom-call(bf16[928,256]{1,0:T(8,128)(2,1)} %x_ref.1, f32[1,256]{1,0:T(1,128)} %bitcast.1), custom_call_target="tpu_custom_call" | custom-call | tf_op jit(solution)/shard_map/pallas_call | solution.py:388
  86.6 3.8 %reshape.7 = f32[1,1,215296]{2,1,0:T(1,128)} reshape(f32[928,232]{1,0:T(8,128)} %shard_map.28) | data formatting | bytes 1722368 | tf_op jit(solution)/shard_map/reshape | solution.py:414

commit v4 on v3

v4 whole, which is shorter than its diff:
```python
import jax
import jax.numpy as jnp
from jax import lax
from jax.experimental import pallas as pl
from jax.experimental.pallas import tpu as pltpu
from jax.sharding import PartitionSpec as P

MEMBERS = 7424
MESH = pl.DeviceIdType.MESH
SENDS = 80


def device(x, y, p, lo, core):
    return (y * 2 + lo, x * 8 + p * 2 + core)


def kernel(
    x_ref, w_ref, out_ref, rows, cols, passing, sums, ysums, table, part, peer,
    row_sem, col_sem, pass_sem, sum_sem, ysum_sem, ztab_sem, xtab_sem, peer_sem, send_sem, load_sem, store_sem,
):
    half = rows.shape[1] // 2
    tile = half // 2
    me_row, me_col = lax.axis_index("mrow"), lax.axis_index("pcol")
    y, lo = me_row // 2, me_row % 2
    x, p, core = me_col // 8, (me_col // 2) % 4, me_col % 2
    hi = p // 2

    xp, xm, x2 = (x + 1) % 4, (x + 3) % 4, (x + 2) % 4
    pp, pm, p2 = (p + 1) % 4, (p + 3) % 4, (p + 2) % 4
    yp, ym, y2 = (y + 1) % 4, (y + 3) % 4, (y + 2) % 4
    x_plus, x_minus, x_far = (device(v, y, p, lo, core) for v in (xp, xm, x2))
    z_plus, z_minus, z_far = (device(x, y, v, lo, core) for v in (pp, pm, p2))
    y_plus, y_minus, y_far = (device(x, v, p, lo, core) for v in (yp, ym, y2))
    z_pair = device(x, y, p, 1 - lo, core)
    twin = device(x, y, p, lo, 1 - core)
    own = x * 4 + p
    diagonal = x == y

    def origin(v):
        return (v + 2 * ((x + v + 1) % 2)) % 4


    turn_lo = [((lo + s - p) % 4) // 2 for s in range(2)]
    turned = [device(x, y, 2 * lo + s, turn_lo[s], core) for s in range(2)]
    stays = [2 * lo + s == p for s in range(2)]
    moves = [jnp.logical_not(v) for v in stays]
    first_p = [(p - hi - 3 * lo) % 4, (p - hi - 1 - lo) % 4]
    second_p = [(p - hi - 3 * (1 - lo)) % 4, (p - hi - 2 + lo) % 4]
    turn_from = [device(x, y, q, hi, core) for q in first_p]
    from_here = [(q == p) & (hi == lo) for q in first_p]
    ahead, behind = hi == lo, hi != lo
    early_p = [jnp.where(ahead, a, b) for a, b in zip(first_p, second_p)]
    late_p = [jnp.where(ahead, b, a) for a, b in zip(first_p, second_p)]

    load = pltpu.make_async_copy(x_ref, rows.at[own], load_sem)
    load.start()
    barrier = pltpu.get_barrier_semaphore()

    def greet(dev):
        pl.semaphore_signal(barrier, inc=1, device_id=dev, device_id_type=MESH)

    for dev in (x_plus, x_minus, x_far, z_plus, z_minus, z_far, y_plus, y_minus, y_far, z_pair, twin):
        greet(dev)
    for s in range(2):
        @pl.when(jnp.logical_not(from_here[s]))
        def _():
            greet(turn_from[s])

    load.wait()
    sums[pl.ds(0, 1)] = jnp.sum(rows[own].astype(jnp.float32), axis=0, keepdims=True)[None]
    pl.semaphore_wait(barrier, 13 - jnp.where(hi == lo, 1, 0))

    sems, sent = {}, {}
    part_of = ["all"]

    def sem_of(name):
        return sems.setdefault(name, len(sems))

    def copy_to(src, dst, recv_sem, dev, n):
        return pltpu.make_async_remote_copy(
            src_ref=src, dst_ref=dst, send_sem=send_sem.at[n], recv_sem=recv_sem,
            device_id=dev, device_id_type=MESH,
        )

    def send(name, src, dst, recv_sem, dev):
        copy_to(src, dst, recv_sem, dev, sem_of(name)).start()
        sent.setdefault(name, set()).add(part_of[0])

    small = []

    def send_small(src, dst, recv_sem, dev):
        copy = copy_to(src, dst, recv_sem, dev, sem_of(("small", len(small))))
        copy.start()
        small.append(copy)

    def arrived(ref, recv_sem):
        copy_to(ref, ref, recv_sem, twin, 0).wait_recv()

    def row_half(i, s):
        return rows.at[i, pl.ds(s * half, half)]

    def send_row(name, i, s, way):
        dev = {"x+": x_plus, "x-": x_minus, "z+": z_plus, "z-": z_minus}[way]
        send((name, s, way), row_half(i, s), row_half(i, s), row_sem.at[i, s], dev)

    def row_arrived(i, s):
        arrived(row_half(i, s), row_sem.at[i, s])

    def send_col(name, i, way):
        dev = {"y+": y_plus, "y-": y_minus, "pair": z_pair}[way]
        send((name, way), cols.at[i], cols.at[i], col_sem.at[i], dev)

    def col_arrived(i):
        arrived(cols.at[i], col_sem.at[i])

    def x_forward(name, q, r):
        i, j = xm * 4 + q, xp * 4 + r
        row_arrived(i, 0)
        send_row(name, i, 0, "x+")
        row_arrived(j, 1)
        send_row(name, j, 1, "x-")

    pushes = []

    def push(src, i, s, dev):
        n = sem_of(("push", len(pushes)))

        @pl.when(diagonal & stays[s])
        def _():
            copy_to(src, cols.at[i], col_sem.at[i], dev, n).start()

        @pl.when(diagonal & moves[s])
        def _():
            copy_to(src, passing.at[s], pass_sem.at[s], dev, n).start()

        pushes.append((src, n))

    def push_row(v, s, dev):
        push(row_half(v * 4 + p, s), v * 4 + p, s, dev)

    turns = []

    def turn_on(s):
        n = sem_of(("turn", s))
        i = origin(y) * 4 + p

        @pl.when(diagonal & moves[s])
        def _():
            copy_to(row_half(x2 * 4 + p, s), cols.at[i], col_sem.at[i], turned[s], n).start()

        @pl.when(diagonal & stays[s])
        def _():
            cols[pl.ds(i, 1)] = rows[pl.ds(x2 * 4 + p, 1), s * half:(s + 1) * half]

        @pl.when(jnp.logical_not(diagonal) & moves[s])
        def _():
            arrived(passing.at[s], pass_sem.at[s])
            copy_to(passing.at[s], cols.at[i], col_sem.at[i], turned[s], n).start()

        turns.append((s, n))

    def to_anomaly(block, i):
        entry = table[i]
        return ((block.astype(jnp.float32) - entry[0:1]) * entry[1:2]).astype(jnp.bfloat16)

    contract = (((1,), (1,)), ((), ()))

    def nth(n, values):
        value = values[0]
        for k in range(1, len(values)):
            value = jnp.where(n == k, values[k], value)
        return value

    def start():
        send_small(sums.at[0], sums.at[1], sum_sem, z_pair)
        send_row("own", own, 0, "x+")
        send_row("own", own, 1, "x-")
        send_row("own", own, 0, "z+")
        send_row("own", own, 1, "z-")
        send_row("own", own, 1, "x+")
        send_row("own", own, 0, "x-")

    def pair_sums():
        arrived(sums.at[1], sum_sem)
        ysums[pl.ds(y, 1)] = (sums[0] + sums[1])[None]
        for dev in (y_plus, y_minus, y_far):
            send_small(ysums.at[y], ysums.at[y], ysum_sem.at[y], dev)
        push_row(x, 0, y_far)
        push_row(x, 1, y_far)

    def means():
        for v in (yp, ym, y2):
            arrived(ysums.at[v], ysum_sem.at[v])
        mean = jnp.sum(ysums[...], axis=0) / MEMBERS
        table[pl.ds(own, 1)] = jnp.concatenate([mean, jnp.sqrt(w_ref[...])], axis=0)[None]
        for dev in (z_plus, z_minus, z_far):
            send_small(table.at[own], table.at[own], ztab_sem.at[p], dev)
        send_row("own", own, 1, "z+")
        send_row("own", own, 0, "z-")

    def x_fwd0():
        x_forward("fwd0", p, p)

    def near_push():
        push_row(xm, 0, y_minus)
        push_row(xp, 1, y_plus)

    def z_first():
        i, j = x * 4 + pm, x * 4 + pp
        row_arrived(i, 0)
        send_row("minus", i, 0, "x+")
        row_arrived(j, 1)
        send_row("plus", j, 1, "x-")
        send_row("plus", j, 1, "x+")
        send_row("minus", i, 0, "x-")

    def z_fwd():
        send_row("minus", x * 4 + pm, 0, "z+")
        send_row("plus", x * 4 + pp, 1, "z-")

    def near_push2():
        row_arrived(xm * 4 + p, 1)
        push_row(xm, 1, y_minus)
        row_arrived(xp * 4 + p, 0)
        push_row(xp, 0, y_plus)

    def tables():
        for q in (pp, pm, p2):
            arrived(table.at[x * 4 + q], ztab_sem.at[q])
        group = table.at[pl.ds(x * 4, 4)]
        for dev in (x_plus, x_minus, x_far):
            send_small(group, group, xtab_sem.at[x], dev)

    def far_rows():
        row_arrived(x2 * 4 + p, 0)
        row_arrived(x2 * 4 + p, 1)

    def z_second():
        i, j = x * 4 + pm, x * 4 + pp
        row_arrived(j, 0)
        send_row("plus", j, 0, "x+")
        row_arrived(i, 1)
        send_row("minus", i, 1, "x-")
        send_row("minus", i, 1, "x+")
        send_row("plus", j, 0, "x-")

    def turn0():
        turn_on(0)

    def turn1():
        turn_on(1)

    def x_fwd1a():
        x_forward("fwd1a", pm, pp)

    def x_fwd1b():
        x_forward("fwd1b", pp, pm)

    def x_fwd2():
        x_forward("fwd2", p2, p2)

    def early(s):
        i = origin(y) * 4 + early_p[s]

        @pl.when(jnp.logical_not(from_here[s] & diagonal))
        def _():
            col_arrived(i)

        if part_of[0] == "ahead":
            send_col(("early", s), i, "pair")
        send_col(("early", s), i, "y+")
        send_col(("early", s), i, "y-")

    def late(s):
        i = origin(y) * 4 + late_p[s]
        col_arrived(i)
        if part_of[0] == "behind":
            send_col(("late", s), i, "pair")
        send_col(("late", s), i, "y+")
        send_col(("late", s), i, "y-")

    def early0():
        early(0)

    def early1():
        early(1)

    def late0():
        late(0)

    def late1():
        late(1)

    def z_far_rows():
        k = x * 4 + p2
        row_arrived(k, 0)
        send_row("far", k, 0, "x+")
        row_arrived(k, 1)
        send_row("far", k, 1, "x-")
        send_row("far", k, 1, "x+")
        send_row("far", k, 0, "x-")

    def tables2():
        for v in (xp, xm, x2):
            arrived(table.at[pl.ds(v * 4, 4)], xtab_sem.at[v])

    def early_fwd():
        i, j = origin(ym) * 4 + early_p[0], origin(yp) * 4 + early_p[1]
        col_arrived(i)
        if part_of[0] == "ahead":
            send_col("early_fwd", i, "y+")
        col_arrived(j)
        if part_of[0] == "ahead":
            send_col("early_fwd", j, "y-")

    def early_pass():
        for s in range(2):
            i = origin(y2) * 4 + early_p[s]
            col_arrived(i)
            if part_of[0] == "ahead":
                send_col(("early_pass", s), i, "pair")

    def late_fwd():
        i, j = origin(ym) * 4 + late_p[0], origin(yp) * 4 + late_p[1]
        col_arrived(i)
        send_col("late_fwd", i, "y+")
        col_arrived(j)
        send_col("late_fwd", j, "y-")

    def rows_rest(q):
        row_arrived(x2 * 4 + q, 0)
        row_arrived(x2 * 4 + q, 1)

    def rows_near():
        for q in (pm, pp):
            row_arrived(xm * 4 + q, 1)
            row_arrived(xp * 4 + q, 0)

    def rows_next():
        rows_rest(pm)
        rows_rest(pp)

    def rows_far():
        row_arrived(xm * 4 + p2, 1)
        row_arrived(xp * 4 + p2, 0)

    e0, e1 = early_p
    l0, l1 = late_p

    def products(blocks, wanted, wait=False):
        def product(n, _):
            i = nth(n, [origin(v) * 4 + q for v, q in blocks])
            if wait:
                col_arrived(i)

            @pl.when(wanted(i // 4, i % 4))
            def _():
                block = to_anomaly(rows[i], i)
                column = to_anomaly(cols[i], i)
                for c in range(2):
                    part[c] += lax.dot_general(
                        block, column[c * tile:(c + 1) * tile], contract,
                        preferred_element_type=jnp.float32,
                    )
            return 0

        lax.fori_loop(0, len(blocks), product, 0)

    def now(v, q):
        return (q != p2) & ((q == p) | (v != x2))

    def next_(v, q):
        return (q != p2) & (q != p) & (v == x2)

    def near(v, q):
        return q != p2

    def far(v, q):
        return (q == p2) & (v != x2)

    own_early, own_late = ((y, e0), (y, e1)), ((y, l0), (y, l1))
    side_early, side_early2 = ((ym, e0), (yp, e1)), ((ym, e1), (yp, e0))
    side_late, side_late2 = ((ym, l0), (yp, l1)), ((ym, l1), (yp, l0))
    far_early, far_late = ((y2, e0), (y2, e1)), ((y2, l0), (y2, l1))

    def clear():
        part[...] = jnp.zeros_like(part)

    def a1():
        for q in (e1, e0):
            col_arrived(origin(ym if q is e1 else yp) * 4 + q)
        rows_near()
        products(own_early + side_early + side_early2 + far_early, now)

    def a2():
        rows_next()
        products(own_early + side_early + side_early2 + far_early, next_)
        products(own_late, near)

    def a3():
        products(side_late, near)

    def b1():
        rows_near()
        products(own_late + own_early, now)

    def b2():
        rows_next()
        products(own_late + own_early, next_)
        products(side_late + side_early, near)

    def b3():
        products(side_late2 + side_early2, near, True)

    def b4():
        products(far_early, near)

    def not_last(v, q):
        return (q != p2) | (v != x2)

    def a_far():
        rows_far()
        products(own_early + side_early + side_early2 + far_early + own_late + side_late, far)

    def a_rest():
        products(side_late2 + far_late, not_last, True)

    def b_far():
        rows_far()
        products(own_early + side_early + side_early2 + far_early + own_late + side_late + side_late2, far)

    def b_rest():
        products(far_late, not_last, True)

    def last():
        i = x2 * 4 + p2
        column = to_anomaly(cols[i], i)
        tiles = column[:tile], column[tile:]
        theirs = jnp.where(core == 0, tiles[1], tiles[0])
        mine = jnp.where(core == 0, tiles[0], tiles[1])

        def halves(s):
            return pl.ds(s * half, half)

        def term(s, right):
            block = to_anomaly(rows[i, s * half:(s + 1) * half], i)
            return lax.dot_general(block, right, contract, preferred_element_type=jnp.float32)

        for s in range(2):
            row_arrived(i, s)
            part[1 - core, halves(s)] += term(s, theirs)
        for s in range(2):
            send_small(part.at[1 - core, halves(s)], peer.at[halves(s)], peer_sem.at[s], twin)
            part[core, halves(s)] += term(s, mine)
        stores = []
        for s in range(2):
            arrived(peer.at[halves(s)], peer_sem.at[s])
            part[core, halves(s)] = (part[core, halves(s)] + peer[halves(s)]) * (1.0 / (MEMBERS - 1))
            stores.append(pltpu.make_async_copy(part.at[core, halves(s)], out_ref.at[halves(s)], store_sem.at[s]))
            stores[s].start()
        for store in stores:
            store.wait()

    def run(steps):
        for step in steps:
            step()

    run((start, pair_sums, means, clear, x_fwd0, near_push, near_push2, z_first, far_rows, turn0, turn1, tables, z_second, x_fwd1a,))

    @pl.when(ahead)
    def _():
        part_of[0] = "ahead"
        run((early0, early1, z_fwd, x_fwd1b, early_fwd, early_pass, tables2, a1, z_far_rows, late0, late1, x_fwd2, a2, late_fwd, a3, a_far, a_rest,))

    @pl.when(behind)
    def _():
        part_of[0] = "behind"
        run((z_fwd, x_fwd1b, early0, late0, late1, early1, z_far_rows, late_fwd, tables2, b1, x_fwd2, early_fwd, b2, b3, early_pass, b4, b_far, b_rest,))

    part_of[0] = "all"
    run((last,))

    for copy in small:
        copy.wait_send()

    def left(name):
        copy_to(cols.at[0], cols.at[0], pass_sem.at[0], twin, sems[name]).wait_send()

    for name, parts in sent.items():
        if parts == {"ahead"}:
            pl.when(ahead)(lambda name=name: left(name))
        elif parts == {"behind"}:
            pl.when(behind)(lambda name=name: left(name))
        else:
            left(name)
    for src, n in pushes:
        @pl.when(diagonal)
        def _():
            copy_to(src, src, pass_sem.at[0], twin, n).wait_send()
    for s, n in turns:
        @pl.when(moves[s])
        def _():
            copy_to(passing.at[s], passing.at[s], pass_sem.at[0], twin, n).wait_send()


def local(snapshots, area_weight):
    members, points = snapshots.shape
    tile = members // 4
    vmem = pl.BlockSpec(memory_space=pltpu.VMEM)
    hbm = pl.BlockSpec(memory_space=pl.ANY)
    dma = pltpu.SemaphoreType.DMA
    gram = pl.pallas_call(
        kernel,
        out_shape=jax.ShapeDtypeStruct((members, tile), jnp.float32),
        in_specs=[hbm, vmem],
        out_specs=hbm,
        scratch_shapes=[
            pltpu.VMEM((16, members, points), jnp.bfloat16),
            pltpu.VMEM((16, members // 2, points), jnp.bfloat16),
            pltpu.VMEM((2, members // 2, points), jnp.bfloat16),
            pltpu.VMEM((2, 1, points), jnp.float32),
            pltpu.VMEM((4, 1, points), jnp.float32),
            pltpu.VMEM((16, 2, points), jnp.float32),
            pltpu.VMEM((2, members, tile), jnp.float32),
            pltpu.VMEM((members, tile), jnp.float32),
            dma((16, 2)),
            dma((16,)),
            dma((2,)),
            dma,
            dma((4,)),
            dma((4,)),
            dma((4,)),
            dma((2,)),
            dma((SENDS,)),
            dma,
            dma((2,)),
        ],
        compiler_params=pltpu.CompilerParams(collective_id=0, has_side_effects=True),
    )(snapshots, area_weight.reshape(1, points))
    return gram.reshape(1, 1, members * tile)


def solution(mesh):
    return jax.shard_map(
        local,
        mesh=mesh,
        in_specs=(P("mrow", "pcol"), P("pcol")),
        out_specs=P("mrow", "pcol", None),
        check_vma=False,
    )
```

time: 90.5 us -> 86.5 us (0.956)
  the two profiles are of different devices: /device:TPU:97 before, /device:TPU:1 now
where the time goes in v4:
time: 86.5 us; the launch traced here: 86.3 us
  Pallas kernels  82.5 us (95%)
  local copies, waits for them, and re-layouts  3.77 us (4%)
    pallas_call x1, Pallas kernels, local(): pl.pallas_call(kernel, out_shape=jax.ShapeDtypeStruct((members, tile), jn...  82.5 us
    reshape x1, local copies, waits for them, and re-layouts, local(): return gram.reshape(1, 1, members * tile)  3.77 us

profile of v4, /device:TPU:1, one launch (start us, length us, event | category | flops | bytes accessed | tf_op | source)
XLA Modules:
  0.0 86.3 jit_solution(13161765699037555579)
XLA Ops:
  0.0 82.5 %shard_map.28 = f32[928,232]{1,0:T(8,128)} custom-call(bf16[928,256]{1,0:T(8,128)(2,1)} %x_ref.1, f32[1,256]{1,0:T(1,128)} %bitcast.1), custom_call_target="tpu_custom_call" | custom-call | tf_op jit(solution)/shard_map/pallas_call | solution.py:512
  82.5 3.8 %reshape.7 = f32[1,1,215296]{2,1,0:T(1,128)} reshape(f32[928,232]{1,0:T(8,128)} %shard_map.28) | data formatting | bytes 1722368 | tf_op jit(solution)/shard_map/reshape | solution.py:540

commit v5 on v4

--- a/solution.py
+++ b/solution.py
@@ -16,7 +16,7 @@
 
 def kernel(
     x_ref, w_ref, out_ref, rows, cols, passing, sums, ysums, table, part, peer,
-    row_sem, col_sem, pass_sem, sum_sem, ysum_sem, ztab_sem, xtab_sem, peer_sem, send_sem, load_sem, store_sem,
+    row_sem, col_sem, pass_sem, sum_sem, ysum_sem, ztab_sem, xtab_sem, peer_sem, send_sem,
 ):
     half = rows.shape[1] // 2
     tile = half // 2
@@ -52,8 +52,6 @@
     early_p = [jnp.where(ahead, a, b) for a, b in zip(first_p, second_p)]
     late_p = [jnp.where(ahead, b, a) for a, b in zip(first_p, second_p)]
 
-    load = pltpu.make_async_copy(x_ref, rows.at[own], load_sem)
-    load.start()
     barrier = pltpu.get_barrier_semaphore()
 
     def greet(dev):
@@ -66,8 +64,7 @@
         def _():
             greet(turn_from[s])
 
-    load.wait()
-    sums[pl.ds(0, 1)] = jnp.sum(rows[own].astype(jnp.float32), axis=0, keepdims=True)[None]
+    sums[pl.ds(0, 1)] = jnp.sum(x_ref[...].astype(jnp.float32), axis=0, keepdims=True)[None]
     pl.semaphore_wait(barrier, 13 - jnp.where(hi == lo, 1, 0))
 
     sems, sent = {}, {}
@@ -105,6 +102,13 @@
 
     def row_arrived(i, s):
         arrived(row_half(i, s), row_sem.at[i, s])
+
+    def own_half(s):
+        return x_ref.at[pl.ds(s * half, half)]
+
+    def send_own(s, way):
+        dev = {"x+": x_plus, "x-": x_minus, "z+": z_plus, "z-": z_minus}[way]
+        send(("own", s, way), own_half(s), row_half(own, s), row_sem.at[own, s], dev)
 
     def send_col(name, i, way):
         dev = {"y+": y_plus, "y-": y_minus, "pair": z_pair}[way]
@@ -173,20 +177,20 @@
 
     def start():
         send_small(sums.at[0], sums.at[1], sum_sem, z_pair)
-        send_row("own", own, 0, "x+")
-        send_row("own", own, 1, "x-")
-        send_row("own", own, 0, "z+")
-        send_row("own", own, 1, "z-")
-        send_row("own", own, 1, "x+")
-        send_row("own", own, 0, "x-")
+        send_own(0, "x+")
+        send_own(1, "x-")
+        send_own(0, "z+")
+        send_own(1, "z-")
+        send_own(1, "x+")
+        send_own(0, "x-")
 
     def pair_sums():
         arrived(sums.at[1], sum_sem)
         ysums[pl.ds(y, 1)] = (sums[0] + sums[1])[None]
         for dev in (y_plus, y_minus, y_far):
             send_small(ysums.at[y], ysums.at[y], ysum_sem.at[y], dev)
-        push_row(x, 0, y_far)
-        push_row(x, 1, y_far)
+        push(own_half(0), own, 0, y_far)
+        push(own_half(1), own, 1, y_far)
 
     def means():
         for v in (yp, ym, y2):
@@ -195,8 +199,8 @@
         table[pl.ds(own, 1)] = jnp.concatenate([mean, jnp.sqrt(w_ref[...])], axis=0)[None]
         for dev in (z_plus, z_minus, z_far):
             send_small(table.at[own], table.at[own], ztab_sem.at[p], dev)
-        send_row("own", own, 1, "z+")
-        send_row("own", own, 0, "z-")
+        send_own(1, "z+")
+        send_own(0, "z-")
 
     def x_fwd0():
         x_forward("fwd0", p, p)
@@ -385,6 +389,7 @@
 
     def clear():
         part[...] = jnp.zeros_like(part)
+        rows[pl.ds(own, 1)] = x_ref[...][None]
 
     def a1():
         for q in (e1, e0):
@@ -452,14 +457,39 @@
         for s in range(2):
             send_small(part.at[1 - core, halves(s)], peer.at[halves(s)], peer_sem.at[s], twin)
             part[core, halves(s)] += term(s, mine)
-        stores = []
         for s in range(2):
             arrived(peer.at[halves(s)], peer_sem.at[s])
-            part[core, halves(s)] = (part[core, halves(s)] + peer[halves(s)]) * (1.0 / (MEMBERS - 1))
-            stores.append(pltpu.make_async_copy(part.at[core, halves(s)], out_ref.at[halves(s)], store_sem.at[s]))
-            stores[s].start()
-        for store in stores:
-            store.wait()
+            out_ref[halves(s)] = (part[core, halves(s)] + peer[halves(s)]) * (1.0 / (MEMBERS - 1))
+
+    def left(name):
+        copy_to(cols.at[0], cols.at[0], pass_sem.at[0], twin, sems[name]).wait_send()
+
+    def made(name, kind):
+        return name not in drained[kind] and bool(sent[name] & {"all", kind})
+
+    drained = {"ahead": set(), "behind": set()}
+
+    def drain(names):
+        for name in names:
+            if made(name, part_of[0]):
+                left(name)
+                drained[part_of[0]].add(name)
+
+    def drain_first():
+        drain([name for name in sent if "all" in sent[name]])
+        for copy in small[:10]:
+            copy.wait_send()
+        for src, n in pushes:
+            @pl.when(diagonal)
+            def _():
+                copy_to(src, src, pass_sem.at[0], twin, n).wait_send()
+        for s, n in turns:
+            @pl.when(moves[s])
+            def _():
+                copy_to(passing.at[s], passing.at[s], pass_sem.at[0], twin, n).wait_send()
+
+    def drain_second():
+        drain([name for name in sent if name[0] not in ("far", "fwd2", ("late", 0), ("late", 1), "late_fwd")])
 
     def run(steps):
         for step in steps:
@@ -470,50 +500,36 @@
     @pl.when(ahead)
     def _():
         part_of[0] = "ahead"
-        run((early0, early1, z_fwd, x_fwd1b, early_fwd, early_pass, tables2, a1, z_far_rows, late0, late1, x_fwd2, a2, late_fwd, a3, a_far, a_rest,))
+        run((early0, early1, z_fwd, x_fwd1b, early_fwd, early_pass, tables2, a1, z_far_rows, late0, late1, x_fwd2, drain_first, a2, late_fwd, a3, a_far, drain_second, a_rest,))
 
     @pl.when(behind)
     def _():
         part_of[0] = "behind"
-        run((z_fwd, x_fwd1b, early0, late0, late1, early1, z_far_rows, late_fwd, tables2, b1, x_fwd2, early_fwd, b2, b3, early_pass, b4, b_far, b_rest,))
+        run((z_fwd, x_fwd1b, early0, late0, late1, early1, z_far_rows, late_fwd, tables2, b1, x_fwd2, drain_first, early_fwd, b2, b3, early_pass, b4, b_far, drain_second, b_rest,))
 
     part_of[0] = "all"
     run((last,))
 
-    for copy in small:
+    for copy in small[10:]:
         copy.wait_send()
-
-    def left(name):
-        copy_to(cols.at[0], cols.at[0], pass_sem.at[0], twin, sems[name]).wait_send()
-
-    for name, parts in sent.items():
-        if parts == {"ahead"}:
-            pl.when(ahead)(lambda name=name: left(name))
-        elif parts == {"behind"}:
-            pl.when(behind)(lambda name=name: left(name))
-        else:
+    for name in sent:
+        kinds = [kind for kind in drained if made(name, kind)]
+        if len(kinds) == 2:
             left(name)
-    for src, n in pushes:
-        @pl.when(diagonal)
-        def _():
-            copy_to(src, src, pass_sem.at[0], twin, n).wait_send()
-    for s, n in turns:
-        @pl.when(moves[s])
-        def _():
-            copy_to(passing.at[s], passing.at[s], pass_sem.at[0], twin, n).wait_send()
+        elif kinds:
+            pl.when(ahead if kinds == ["ahead"] else behind)(lambda name=name: left(name))
 
 
 def local(snapshots, area_weight):
     members, points = snapshots.shape
     tile = members // 4
     vmem = pl.BlockSpec(memory_space=pltpu.VMEM)
-    hbm = pl.BlockSpec(memory_space=pl.ANY)
     dma = pltpu.SemaphoreType.DMA
     gram = pl.pallas_call(
         kernel,
         out_shape=jax.ShapeDtypeStruct((members, tile), jnp.float32),
-        in_specs=[hbm, vmem],
-        out_specs=hbm,
+        in_specs=[vmem, vmem],
+        out_specs=vmem,
         scratch_shapes=[
             pltpu.VMEM((16, members, points), jnp.bfloat16),
             pltpu.VMEM((16, members // 2, points), jnp.bfloat16),
@@ -532,10 +548,10 @@
             dma((4,)),
             dma((2,)),
             dma((SENDS,)),
-            dma,
-            dma((2,)),
         ],
-        compiler_params=pltpu.CompilerParams(collective_id=0, has_side_effects=True),
+        compiler_params=pltpu.CompilerParams(
+            collective_id=0, has_side_effects=True, vmem_limit_bytes=24 * 1024 * 1024
+        ),
     )(snapshots, area_weight.reshape(1, points))
     return gram.reshape(1, 1, members * tile)
 

time: 86.5 us -> 85.3 us (0.986)
  Pallas kernels: 82.5 us -> 80.9 us
    unnamed x0 -> x4, local copies, waits for them, and re-layouts: none -> 1.7 us
    pallas_call x1, Pallas kernels: 82.5 us -> 80.9 us  [local(): pl.pallas_call(kernel, out_shape=jax.ShapeDtypeStruct((members, tile), jn...]
    reshape x1, local copies, waits for them, and re-layouts: 3.77 us -> 2.57 us  [local(): return gram.reshape(1, 1, members * tile)]
where the time goes in v5:
time: 85.3 us; the launch traced here: 85.2 us
  Pallas kernels  80.9 us (95%)
  local copies, waits for them, and re-layouts  4.27 us (5%)
    pallas_call x1, Pallas kernels, local(): pl.pallas_call(kernel, out_shape=jax.ShapeDtypeStruct((members, tile), jn...  80.9 us
    reshape x1, local copies, waits for them, and re-layouts, local(): return gram.reshape(1, 1, members * tile)  2.57 us

profile of v5, /device:TPU:1, one launch (start us, length us, event | category | flops | bytes accessed | tf_op | source)
XLA Modules:
  0.0 85.2 jit_solution(16801345532985204197)
XLA Ops:
  0.0 0.0 copy-start.1
  0.0 0.7 copy-done.1
  0.7 0.0 copy-start
  0.7 1.0 %copy-done = bf16[928,256]{1,0:T(8,128)(2,1)S(1)} copy-done((bf16[928,256]{1,0:T(8,128)(2,1)S(1)}, bf16[928,256]{1,0:T(8,128)(2,1)}, u32[]{:S(2)}) %copy-start) | copy-done | bytes 475160
  1.7 80.9 %shard_map.28 = f32[928,232]{1,0:T(8,128)S(1)} custom-call(bf16[928,256]{1,0:T(8,128)(2,1)S(1)} %copy-done, f32[1,256]{1,0:T(1,128)S(1)} %bitcast.1), custom_call_target="tpu_custom_call" | custom-call | tf_op jit(solution)/shard_map/pallas_call | solution.py:528
  82.6 2.6 %reshape.7 = f32[1,1,215296]{2,1,0:T(1,128)} reshape(f32[928,232]{1,0:T(8,128)S(1)} %shard_map.28) | data formatting | bytes 1722368 | tf_op jit(solution)/shard_map/reshape | solution.py:556
Async XLA Ops:
  0.0 0.7 copy-start.1
  0.7 1.0 %copy-start = (bf16[928,256]{1,0:T(8,128)(2,1)S(1)}, bf16[928,256]{1,0:T(8,128)(2,1)}, u32[]{:S(2)}) copy-start(bf16[928,256]{1,0:T(8,128)(2,1)} %x_ref.1) | copy-start | bytes 1425412

commit v6 on v5

--- a/solution.py
+++ b/solution.py
@@ -7,7 +7,7 @@
 
 MEMBERS = 7424
 MESH = pl.DeviceIdType.MESH
-SENDS = 80
+SENDS = 18
 
 
 def device(x, y, p, lo, core):
@@ -67,11 +67,9 @@
     sums[pl.ds(0, 1)] = jnp.sum(x_ref[...].astype(jnp.float32), axis=0, keepdims=True)[None]
     pl.semaphore_wait(barrier, 13 - jnp.where(hi == lo, 1, 0))
 
-    sems, sent = {}, {}
+    FIRST, SECOND, THIRD, PUSH, TURN, SMALL = 0, 1, 2, 3, 4, 6
+    started = {}
     part_of = ["all"]
-
-    def sem_of(name):
-        return sems.setdefault(name, len(sems))
 
     def copy_to(src, dst, recv_sem, dev, n):
         return pltpu.make_async_remote_copy(
@@ -80,13 +78,23 @@
         )
 
     def send(name, src, dst, recv_sem, dev):
-        copy_to(src, dst, recv_sem, dev, sem_of(name)).start()
-        sent.setdefault(name, set()).add(part_of[0])
+        if part_of[0] == "all":
+            n = FIRST
+        elif name[0] in ("far", "fwd2", ("late", 0), ("late", 1), "late_fwd"):
+            n = THIRD
+        else:
+            n = SECOND
+        copy_to(src, dst, recv_sem, dev, n).start()
+        started[part_of[0], n] = started.get((part_of[0], n), 0) + 1
+
+    def all_left(n, halves):
+        blocks = rows.at[pl.ds(0, halves // 2)]
+        copy_to(blocks, blocks, pass_sem.at[0], twin, n).wait_send()
 
     small = []
 
     def send_small(src, dst, recv_sem, dev):
-        copy = copy_to(src, dst, recv_sem, dev, sem_of(("small", len(small))))
+        copy = copy_to(src, dst, recv_sem, dev, SMALL + len(small))
         copy.start()
         small.append(copy)
 
@@ -127,7 +135,7 @@
     pushes = []
 
     def push(src, i, s, dev):
-        n = sem_of(("push", len(pushes)))
+        n = PUSH
 
         @pl.when(diagonal & stays[s])
         def _():
@@ -145,7 +153,7 @@
     turns = []
 
     def turn_on(s):
-        n = sem_of(("turn", s))
+        n = TURN + s
         i = origin(y) * 4 + p
 
         @pl.when(diagonal & moves[s])
@@ -461,35 +469,22 @@
             arrived(peer.at[halves(s)], peer_sem.at[s])
             out_ref[halves(s)] = (part[core, halves(s)] + peer[halves(s)]) * (1.0 / (MEMBERS - 1))
 
-    def left(name):
-        copy_to(cols.at[0], cols.at[0], pass_sem.at[0], twin, sems[name]).wait_send()
-
-    def made(name, kind):
-        return name not in drained[kind] and bool(sent[name] & {"all", kind})
-
-    drained = {"ahead": set(), "behind": set()}
-
-    def drain(names):
-        for name in names:
-            if made(name, part_of[0]):
-                left(name)
-                drained[part_of[0]].add(name)
-
     def drain_first():
-        drain([name for name in sent if "all" in sent[name]])
+        all_left(FIRST, started["all", FIRST])
         for copy in small[:10]:
             copy.wait_send()
-        for src, n in pushes:
-            @pl.when(diagonal)
-            def _():
-                copy_to(src, src, pass_sem.at[0], twin, n).wait_send()
+
+        @pl.when(diagonal)
+        def _():
+            all_left(PUSH, len(pushes))
+
         for s, n in turns:
             @pl.when(moves[s])
             def _():
                 copy_to(passing.at[s], passing.at[s], pass_sem.at[0], twin, n).wait_send()
 
     def drain_second():
-        drain([name for name in sent if name[0] not in ("far", "fwd2", ("late", 0), ("late", 1), "late_fwd")])
+        all_left(SECOND, started[part_of[0], SECOND])
 
     def run(steps):
         for step in steps:
@@ -512,12 +507,14 @@
 
     for copy in small[10:]:
         copy.wait_send()
-    for name in sent:
-        kinds = [kind for kind in drained if made(name, kind)]
-        if len(kinds) == 2:
-            left(name)
-        elif kinds:
-            pl.when(ahead if kinds == ["ahead"] else behind)(lambda name=name: left(name))
+
+    @pl.when(ahead)
+    def _():
+        all_left(THIRD, started["ahead", THIRD])
+
+    @pl.when(behind)
+    def _():
+        all_left(THIRD, started["behind", THIRD])
 
 
 def local(snapshots, area_weight):

time: 85.3 us -> 84.8 us (level)
  no operation moved by 1% of the time
where the time goes in v6:
time: 84.8 us; the launch traced here: 84.7 us
  Pallas kernels  80.4 us (95%)
  local copies, waits for them, and re-layouts  4.27 us (5%)
    pallas_call x1, Pallas kernels, local(): pl.pallas_call(kernel, out_shape=jax.ShapeDtypeStruct((members, tile), jn...  80.4 us
    reshape x1, local copies, waits for them, and re-layouts, local(): return gram.reshape(1, 1, members * tile)  2.57 us
    unnamed x4, local copies, waits for them, and re-layouts  1.7 us

profile of v6, /device:TPU:1, one launch (start us, length us, event | category | flops | bytes accessed | tf_op | source)
XLA Modules:
  0.0 84.7 jit_solution(4355282782058566563)
XLA Ops:
  0.0 0.0 copy-start.1
  0.0 0.7 copy-done.1
  0.7 0.0 copy-start
  0.7 1.0 %copy-done = bf16[928,256]{1,0:T(8,128)(2,1)S(1)} copy-done((bf16[928,256]{1,0:T(8,128)(2,1)S(1)}, bf16[928,256]{1,0:T(8,128)(2,1)}, u32[]{:S(2)}) %copy-start) | copy-done | bytes 475160
  1.7 80.4 %shard_map.28 = f32[928,232]{1,0:T(8,128)S(1)} custom-call(bf16[928,256]{1,0:T(8,128)(2,1)S(1)} %copy-done, f32[1,256]{1,0:T(1,128)S(1)} %bitcast.1), custom_call_target="tpu_custom_call" | custom-call | tf_op jit(solution)/shard_map/pallas_call | solution.py:525
  82.1 2.6 %reshape.7 = f32[1,1,215296]{2,1,0:T(1,128)} reshape(f32[928,232]{1,0:T(8,128)S(1)} %shard_map.28) | data formatting | bytes 1722368 | tf_op jit(solution)/shard_map/reshape | solution.py:553
Async XLA Ops:
  0.0 0.7 copy-start.1
  0.7 1.0 %copy-start = (bf16[928,256]{1,0:T(8,128)(2,1)S(1)}, bf16[928,256]{1,0:T(8,128)(2,1)}, u32[]{:S(2)}) copy-start(bf16[928,256]{1,0:T(8,128)(2,1)} %x_ref.1) | copy-start | bytes 1425412

commit v7 on v6

--- a/solution.py
+++ b/solution.py
@@ -490,7 +490,7 @@
         for step in steps:
             step()
 
-    run((start, pair_sums, means, clear, x_fwd0, near_push, near_push2, z_first, far_rows, turn0, turn1, tables, z_second, x_fwd1a,))
+    run((start, pair_sums, means, clear, x_fwd0, near_push, near_push2, z_first, far_rows, turn1, turn0, tables, z_second, x_fwd1a,))
 
     @pl.when(ahead)
     def _():

time: 84.8 us -> 83.7 us (0.987); the launches traced: 84.7 us -> 82.1 us
  Pallas kernels: 80.4 us -> 77.8 us
    pallas_call x1, Pallas kernels: 80.4 us -> 77.8 us  [local(): pl.pallas_call(kernel, out_shape=jax.ShapeDtypeStruct((members, tile), jn...]
where the time goes in v7:
time: 83.7 us; the launch traced here: 82.1 us
  Pallas kernels  77.8 us (93%)
  local copies, waits for them, and re-layouts  4.27 us (5%)
    pallas_call x1, Pallas kernels, local(): pl.pallas_call(kernel, out_shape=jax.ShapeDtypeStruct((members, tile), jn...  77.8 us
    reshape x1, local copies, waits for them, and re-layouts, local(): return gram.reshape(1, 1, members * tile)  2.57 us
    unnamed x4, local copies, waits for them, and re-layouts  1.7 us

profile of v7, /device:TPU:1, one launch (start us, length us, event | category | flops | bytes accessed | tf_op | source)
XLA Modules:
  0.0 82.1 jit_solution(14910149609464139526)
XLA Ops:
  0.0 0.0 copy-start.1
  0.0 0.7 copy-done.1
  0.7 0.0 copy-start
  0.7 1.0 %copy-done = bf16[928,256]{1,0:T(8,128)(2,1)S(1)} copy-done((bf16[928,256]{1,0:T(8,128)(2,1)S(1)}, bf16[928,256]{1,0:T(8,128)(2,1)}, u32[]{:S(2)}) %copy-start) | copy-done | bytes 475160
  1.7 77.8 %shard_map.28 = f32[928,232]{1,0:T(8,128)S(1)} custom-call(bf16[928,256]{1,0:T(8,128)(2,1)S(1)} %copy-done, f32[1,256]{1,0:T(1,128)S(1)} %bitcast.1), custom_call_target="tpu_custom_call" | custom-call | tf_op jit(solution)/shard_map/pallas_call | solution.py:525
  79.5 2.6 %reshape.7 = f32[1,1,215296]{2,1,0:T(1,128)} reshape(f32[928,232]{1,0:T(8,128)S(1)} %shard_map.28) | data formatting | bytes 1722368 | tf_op jit(solution)/shard_map/reshape | solution.py:553
Async XLA Ops:
  0.0 0.7 copy-start.1
  0.7 1.0 %copy-start = (bf16[928,256]{1,0:T(8,128)(2,1)S(1)}, bf16[928,256]{1,0:T(8,128)(2,1)}, u32[]{:S(2)}) copy-start(bf16[928,256]{1,0:T(8,128)(2,1)} %x_ref.1) | copy-start | bytes 1425412

commit v8 on v7

--- a/solution.py
+++ b/solution.py
@@ -495,7 +495,7 @@
     @pl.when(ahead)
     def _():
         part_of[0] = "ahead"
-        run((early0, early1, z_fwd, x_fwd1b, early_fwd, early_pass, tables2, a1, z_far_rows, late0, late1, x_fwd2, drain_first, a2, late_fwd, a3, a_far, drain_second, a_rest,))
+        run((early0, early1, z_fwd, x_fwd1b, early_fwd, early_pass, tables2, a1, z_far_rows, late0, late1, x_fwd2, drain_first, late_fwd, a2, a3, a_far, drain_second, a_rest,))
 
     @pl.when(behind)
     def _():

time: 83.7 us -> 83.7 us (level)
  no operation moved by 1% of the time
where the time goes in v8:
time: 83.7 us; the launch traced here: 82.1 us
  Pallas kernels  77.8 us (93%)
  local copies, waits for them, and re-layouts  4.27 us (5%)
    pallas_call x1, Pallas kernels, local(): pl.pallas_call(kernel, out_shape=jax.ShapeDtypeStruct((members, tile), jn...  77.8 us
    reshape x1, local copies, waits for them, and re-layouts, local(): return gram.reshape(1, 1, members * tile)  2.57 us
    unnamed x4, local copies, waits for them, and re-layouts  1.7 us

profile of v8, /device:TPU:1, one launch (start us, length us, event | category | flops | bytes accessed | tf_op | source)
XLA Modules:
  0.0 82.1 jit_solution(4380930135110650764)
XLA Ops:
  0.0 0.0 copy-start.1
  0.0 0.7 copy-done.1
  0.7 0.0 copy-start
  0.7 1.0 %copy-done = bf16[928,256]{1,0:T(8,128)(2,1)S(1)} copy-done((bf16[928,256]{1,0:T(8,128)(2,1)S(1)}, bf16[928,256]{1,0:T(8,128)(2,1)}, u32[]{:S(2)}) %copy-start) | copy-done | bytes 475160
  1.7 77.8 %shard_map.28 = f32[928,232]{1,0:T(8,128)S(1)} custom-call(bf16[928,256]{1,0:T(8,128)(2,1)S(1)} %copy-done, f32[1,256]{1,0:T(1,128)S(1)} %bitcast.1), custom_call_target="tpu_custom_call" | custom-call | tf_op jit(solution)/shard_map/pallas_call | solution.py:525
  79.5 2.6 %reshape.7 = f32[1,1,215296]{2,1,0:T(1,128)} reshape(f32[928,232]{1,0:T(8,128)S(1)} %shard_map.28) | data formatting | bytes 1722368 | tf_op jit(solution)/shard_map/reshape | solution.py:553
Async XLA Ops:
  0.0 0.7 copy-start.1
  0.7 1.0 %copy-start = (bf16[928,256]{1,0:T(8,128)(2,1)S(1)}, bf16[928,256]{1,0:T(8,128)(2,1)}, u32[]{:S(2)}) copy-start(bf16[928,256]{1,0:T(8,128)(2,1)} %x_ref.1) | copy-start | bytes 1425412
